TPU v7x, 256 devices: a whole 4x4x8 slice. The times are simulated.
256 devices in a mesh: ctx: 8 (over z), vocab: 32 (over y, x, core).
Axes of the slice: x: 4, y: 4, z: 8, core: 2. Of those that a mesh axis runs over, the one named last changes fastest.
Arguments:
- hidden: bfloat16 [16, 128, 4096], P(None, 'ctx', 'vocab'), may hold values from -6 to 6
- head_weight: bfloat16 [4096, 128256], P(None, ('ctx', 'vocab')), may hold values from -0.09375 to 0.09375
- token_ids: int32 [16, 128], P(None, 'ctx'), may hold values from 0 to 128255
- response_mask: int32 [16, 128], P(None, 'ctx'), may hold values 0 or 1
- pair_order: int32 [16], replicated, may hold values from 0 to 15, each once
- frozen_logprob: float32 [16], replicated, may hold values from -40 to 40
Outputs:
- pair_loss: float32 [], replicated
- margins: float32 [8], replicated
- head_grad: bfloat16 [4096, 128256], P(None, ('ctx', 'vocab'))
- spread_grad: bfloat16 [4096, 128256], P(None, ('ctx', 'vocab'))
Inputs may be any that keep to these rules, and one draw needn't show every extreme that they name: `token_ids`: token ids lie in 0 to 128255. `response_mask`: mask entries are 0 or 1. pair_order names every sequence exactly once; entry p is the chosen sequence of pair p and entry 8 + p the rejected one.
All inputs are finite; a program needn't handle non-finite values.
Results may differ from a plain program's by a relative error of at most 0.0015.
Values may be sent and summed in bfloat16 or wider, within the bound.
A program may use at most 128 MiB of HBM per device.

v0:
```python
import jax
import jax.numpy as jnp
from jax import lax
from jax.sharding import Mesh
from jax.sharding import PartitionSpec as P

V = 128256
VOCAB = ("vocab_0", "vocab_1", "vocab_2")
CTX_VOCAB = ("ctx", "vocab_0", "vocab_1", "vocab_2")


strength = 0.1
loss_scale = 256.0


def laid_out(pieces, dim):
    pieces = jnp.moveaxis(pieces, 0, dim)
    lengths = pieces.shape
    return pieces.reshape(*lengths[:dim], lengths[dim] * lengths[dim + 1], *lengths[dim + 2 :])


def gather_packed(arrays, axis, dims):
    flat = jnp.concatenate([a.reshape(-1) for a in arrays])
    lines, at, finished = lax.all_gather(flat, axis), 0, []
    for a, dim in zip(arrays, dims):
        pieces = lines[:, at : at + a.size].reshape(-1, *a.shape)
        finished.append(laid_out(pieces, dim))
        at += a.size
    return tuple(finished)


def by_axis(shard, axes):
    for axis in axes:
        shard = lax.pmax(shard, axis)
    return shard


def by_axis_2(shard, axes):
    for axis in axes:
        shard = lax.psum(shard, axis)
    return shard


def contract_rows(block_rows, both_logits):
    return lax.dot_general(
        block_rows, both_logits, (((0,), (0,)), ((), ())), preferred_element_type=jnp.float32
    )


def shards(hidden, head_weight, token_ids, response_mask, pair_order, frozen_logprob):
    seq_rows = lax.all_gather(hidden, "ctx", axis=1, tiled=True)
    ids_all, mask_all = gather_packed((token_ids, response_mask), "ctx", (1, 1))
    token_rows = seq_rows.reshape(seq_rows.shape[0] * seq_rows.shape[1], seq_rows.shape[2])
    shard_width = head_weight.shape[1]
    whole_rows = lax.all_gather(token_rows, VOCAB, axis=1, tiled=True)
    logits = jnp.dot(whole_rows, head_weight, preferred_element_type=jnp.float32)
    offset = lax.axis_index(CTX_VOCAB) * shard_width
    local_ids = ids_all.reshape(-1) - offset
    columns = jnp.arange(shard_width).astype(jnp.int32)
    onehot = (columns[None, :] == local_ids[:, None]).astype(jnp.float32)
    picked_part = jnp.sum(onehot * logits, axis=1)
    peak_part = jnp.max(logits, axis=1)
    row_peak = by_axis(peak_part, CTX_VOCAB)
    exp_sums = jnp.sum(jnp.exp(logits - row_peak[:, None]), axis=1)
    sum_total, picked = (by_axis_2(exp_sums, CTX_VOCAB), by_axis_2(picked_part, CTX_VOCAB))
    log_norm = row_peak + jnp.log(sum_total)
    mask_flat = mask_all.reshape(-1).astype(jnp.float32)
    seq_count = ids_all.shape[0]
    policy = jnp.sum(((picked - log_norm) * mask_flat).reshape(seq_count, ids_all.shape[1]), axis=1)
    log_ratio = policy - frozen_logprob
    pair_count = pair_order.shape[0] // 2
    chosen = pair_order[:pair_count]
    rejected = pair_order[pair_count:]
    margins = strength * (log_ratio[chosen] - log_ratio[rejected])
    pair_loss = jnp.mean(jax.nn.softplus(-margins))
    weight = -loss_scale * strength * jax.nn.sigmoid(-margins) / pair_count
    seq_coef = jnp.zeros((seq_count,), jnp.float32).at[chosen].set(weight).at[rejected].set(-weight)
    token_coef = (seq_coef[:, None] * mask_all.astype(jnp.float32)).reshape(-1)
    probabilities = jnp.exp(logits - log_norm[:, None])
    grad_logits = (token_coef[:, None] * (onehot - probabilities)).astype(jnp.bfloat16)
    spread_logits = (V / 64.0 * token_coef[:, None] * probabilities).astype(jnp.bfloat16)
    both_logits = jnp.concatenate([grad_logits, spread_logits], axis=1)
    both_grads = contract_rows(whole_rows, both_logits)
    head_grad = both_grads[:, :shard_width].astype(jnp.bfloat16)
    spread_grad = both_grads[:, shard_width:].astype(jnp.bfloat16)
    return (pair_loss, margins, head_grad, spread_grad)


def solution(mesh):
    split = Mesh(
        mesh.devices.reshape(mesh.shape["ctx"], 4, 4, 2), ("ctx", "vocab_0", "vocab_1", "vocab_2")
    )
    placed = (P(None, "ctx", VOCAB), P(None, CTX_VOCAB), P(None, "ctx"), P(None, "ctx"), P(), P())
    return jax.shard_map(
        shards,
        mesh=split,
        in_specs=placed,
        out_specs=(P(), P(), P(None, CTX_VOCAB), P(None, CTX_VOCAB)),
        check_vma=False,
    )
```

profile of v0, /device:TPU:1, one launch (start us, length us, event | category | flops | bytes accessed | tf_op | source)
XLA Modules:
  0.0 281.2 jit_solution(17380326910799111413)
XLA Ops:
  7.2 0.0 all-gather.4.cloned.1.call-start
  7.2 26.5 %all_gather.14 = bf16[16,128,128]{2,1,0:T(8,128)(2,1)} all-gather(bf16[16,16,128]{2,1,0:T(8,128)(2,1)} %param.6), channel_id=1, replica_groups=mesh['ctx'=8,'vocab_0'=4,'vocab_1'=4,'vocab_2'=2] {'ctx'}, dimensions={1}, use_global_device_ids=true | all-gather | bytes 589824 | tf_op jit(solution)/shard_map/all_gather | solution.py:51
  33.7 0.0 all-gather.4.cloned.1.call-update
  33.7 0.8 reshape.60
  34.5 0.8 reshape.61
  35.3 18.1 %all-gather.1 = s32[8,1,512]{2,1,0:T(1,128)S(1)} all-gather(s32[1,1,512]{2,1,0:T(1,128)S(1)} %bitcast.21), channel_id=2, replica_groups=mesh['ctx'=8,'vocab_0'=4,'vocab_1'=4,'vocab_2'=2] {'ctx'}, dimensions={0}, use_global_device_ids=true | all-gather | bytes 18432 | tf_op jit(solution)/shard_map/all_gather | solution.py:24
  53.4 0.1 sub.49
  53.6 0.1 sub.51
  53.6 0.1 convert_element_type.33
  53.8 0.1 convert_element_type.35
  53.8 0.8 compare_select_fusion.1
  54.6 68.8 %all-gather.4.cloned.1.call-done = bf16[2048,4096]{1,0:T(8,128)(2,1)} async-done(((bf16[2048,128]{1,0:T(8,128)(2,1)}), bf16[2048,4096]{1,0:T(8,128)(2,1)}) %all-gather.4.cloned.1.call-update) | async-done | bytes 16777232 | tf_op jit(solution)/shard_map/all_gather | solution.py:55
  123.5 14.8 %fusion.9 = (f32[2048]{0:T(1024)S(1)}, f32[2048,501]{0,1:T(8,128)}) fusion(bf16[2048,4096]{1,0:T(8,128)(2,1)} %all-gather.4.cloned.1.call-done, bf16[4096,501]{0,1:T(8,128)(2,1)} %param.7), kind=kOutput, calls=%fused_computation.35 | convolution fusion | flops 8406409216 | bytes 24993792 | tf_op jit(solution)/shard_map/dot_general | solution.py:56
  138.3 0.0 copy-start.1
  138.3 14.1 %pmax.28 = f32[2048]{0:T(1024)S(1)} all-reduce(f32[2048]{0:T(1024)S(1)} %get-tuple-element.29), channel_id=1, replica_groups=mesh['ctx'=8,'vocab_0'=4,'vocab_1'=4,'vocab_2'=2] {'ctx'}, use_global_device_ids=true, to_apply=%region_6.0 | all-reduce | flops 2048 | bytes 16384 | tf_op jit(solution)/shard_map/pmax | solution.py:34
  152.3 8.2 %pmax.29 = f32[2048]{0:T(1024)S(1)} all-reduce(f32[2048]{0:T(1024)S(1)} %pmax.28), channel_id=1, replica_groups=mesh['ctx'=8,'vocab_0'=4,'vocab_1'=4,'vocab_2'=2] {'vocab_0'}, use_global_device_ids=true, to_apply=%region_7.0 | all-reduce | flops 2048 | bytes 16384 | tf_op jit(solution)/shard_map/pmax | solution.py:34
  160.6 7.4 %pmax.30 = f32[2048]{0:T(1024)S(1)} all-reduce(f32[2048]{0:T(1024)S(1)} %pmax.29), channel_id=1, replica_groups=mesh['ctx'=8,'vocab_0'=4,'vocab_1'=4,'vocab_2'=2] {'vocab_1'}, use_global_device_ids=true, to_apply=%region_8.0 | all-reduce | flops 2048 | bytes 16384 | tf_op jit(solution)/shard_map/pmax | solution.py:34
  167.9 10.1 %pmax.31 = f32[2048]{0:T(1024)S(1)} all-reduce(f32[2048]{0:T(1024)S(1)} %pmax.30), channel_id=1, replica_groups=mesh['ctx'=8,'vocab_0'=4,'vocab_1'=4,'vocab_2'=2] {'vocab_2'}, use_global_device_ids=true, to_apply=%region_9.0 | all-reduce | flops 2048 | bytes 16384 | tf_op jit(solution)/shard_map/pmax | solution.py:34
  178.0 3.3 %exponential_reduce_fusion = (f32[2048]{0:T(1024)S(1)}, f32[2048]{0:T(1024)S(1)}) fusion(f32[2048,501]{0,1:T(8,128)} %get-tuple-element.30, f32[2048]{0:T(1024)S(1)} %pmax.31, s32[2048]{0:T(1024)S(1)} %sub.51), kind=kLoop, calls=%fused_computation.11 | loop fusion | flops 5126144 | bytes 4136960 | tf_op jit(solution)/shard_map/reduce_sum | solution.py:64
  181.3 20.5 %all-reduce = (f32[2048]{0:T(1024)S(1)}, f32[2048]{0:T(1024)S(1)}) all-reduce(f32[2048]{0:T(1024)S(1)} %get-tuple-element.5, f32[2048]{0:T(1024)S(1)} %get-tuple-element.4), channel_id=1, replica_groups=mesh['ctx'=8,'vocab_0'=4,'vocab_1'=4,'vocab_2'=2] {'ctx'}, use_global_device_ids=true, to_apply=%region_1.0 | all-reduce | flops 4096 | bytes 32768 | tf_op jit(solution)/shard_map/psum | solution.py:40
  201.8 10.8 %all-reduce.2 = (f32[2048]{0:T(1024)S(1)}, f32[2048]{0:T(1024)S(1)}) all-reduce(f32[2048]{0:T(1024)S(1)} %get-tuple-element.6, f32[2048]{0:T(1024)S(1)} %get-tuple-element.7), channel_id=1, replica_groups=mesh['ctx'=8,'vocab_0'=4,'vocab_1'=4,'vocab_2'=2] {'vocab_0'}, use_global_device_ids=true, to_apply=%region_2.0 | all-reduce | flops 4096 | bytes 32768 | tf_op jit(solution)/shard_map/psum | solution.py:40
  212.6 10.8 %all-reduce.1 = (f32[2048]{0:T(1024)S(1)}, f32[2048]{0:T(1024)S(1)}) all-reduce(f32[2048]{0:T(1024)S(1)} %get-tuple-element.10, f32[2048]{0:T(1024)S(1)} %get-tuple-element.11), channel_id=1, replica_groups=mesh['ctx'=8,'vocab_0'=4,'vocab_1'=4,'vocab_2'=2] {'vocab_1'}, use_global_device_ids=true, to_apply=%region_3.0 | all-reduce | flops 4096 | bytes 32768 | tf_op jit(solution)/shard_map/psum | solution.py:40
  223.5 17.9 %all-reduce.3 = (f32[2048]{0:T(1024)S(1)}, f32[2048]{0:T(1024)S(1)}) all-reduce(f32[2048]{0:T(1024)S(1)} %get-tuple-element.8, f32[2048]{0:T(1024)S(1)} %get-tuple-element.9), channel_id=1, replica_groups=mesh['ctx'=8,'vocab_0'=4,'vocab_1'=4,'vocab_2'=2] {'vocab_2'}, use_global_device_ids=true, to_apply=%region_4.0 | all-reduce | flops 4096 | bytes 32768 | tf_op jit(solution)/shard_map/psum | solution.py:40
  241.4 0.1 bitcast_reduce_fusion
  241.5 0.0 copy-done.1
  241.6 0.6 gather_fusion.1
  242.2 0.6 gather_fusion
  242.9 0.0 copy-start
  242.9 0.6 scatter_custom_fusion
  243.5 0.8 scatter_fusion
  244.3 0.1 broadcast_multiply_fusion
  244.3 3.5 %multiply_convert_fusion.1 = (bf16[2048,501]{0,1:T(8,128)(2,1)S(1)}, bf16[2048,501]{0,1:T(8,128)(2,1)S(1)}) fusion(f32[2048,501]{0,1:T(8,128)} %get-tuple-element.30, f32[2048]{0:T(1024)S(1)} %get-tuple-element.20, f32[2048]{0:T(1024)S(1)} %get-tuple-element.15, s32[2048]{0:T(1024)S(1)} %sub.51, f32[2048]{0:T(1024)S(1)} %get-tuple-element.14), kind=kLoop, calls=%fused_computation.9 | loop fusion | flops 8208384 | bytes 8241152 | tf_op jit(solution)/shard_map/convert_element_type | solution.py:80
  247.9 20.1 %convert_bitcast_fusion = bf16[4096,1002]{0,1:T(8,128)(2,1)S(1)} fusion(bf16[2048,4096]{1,0:T(8,128)(2,1)} %all-gather.4.cloned.1.call-done, bf16[2048,501]{0,1:T(8,128)(2,1)S(1)} %get-tuple-element.24, bf16[2048,501]{0,1:T(8,128)(2,1)S(1)} %get-tuple-element.23), kind=kOutput, calls=%fused_computation.4 | convolution fusion | flops 16823083008 | bytes 29089792 | tf_op jit(solution)/shard_map/dot_general | solution.py:45
  267.9 4.0 %fusion.8 = (bf16[4096,501]{0,1:T(8,128)(2,1)}, bf16[4096,501]{0,1:T(8,128)(2,1)}) fusion(bf16[4096,1002]{0,1:T(8,128)(2,1)S(1)} %convert_bitcast_fusion), kind=kLoop, calls=%fused_computation.34 | loop fusion | bytes 16416768 | tf_op jit(solution)/shard_map/slice | solution.py:85
  272.0 0.0 copy-done
  272.0 0.6 fusion.3
  (8 shorter events, 0.1 us)
Async XLA Ops:
  7.2 116.3 %all-gather.4.cloned.1.call-start = ((), (), s32[]{:S(2)}) async-start(), calls=%async_computation | async-start | bytes 17301504 | tf_op jit(solution)/shard_map/all_gather | solution.py:55
  138.3 103.3 %copy-start.1 = (f32[16]{0:T(128)S(1)}, f32[16]{0:T(128)}, u32[]{:S(2)}) copy-start(f32[16]{0:T(128)} %param.11) | copy-start | bytes 196
  242.9 29.1 %copy-start = (f32[8]{0:T(128)}, f32[8]{0:T(128)S(1)}, u32[]{:S(2)}) copy-start(f32[8]{0:T(128)S(1)} %get-tuple-element.18) | copy-start | bytes 100
Sparse Core Ops, SparseCore 0:
  33.8 89.5 all-gather.3
where the time goes:
time: 282 us; the launch traced here: 281 us
  blocking collectives  144 us (51%)
  waiting for transfers between devices  68.8 us (24%)
  matrix products  34.9 us (12%)
  between operations  15.9 us (6%)
  local copies, waits for them, and re-layouts  8.6 us (3%)
  other arithmetic  8.44 us (3%)
    all_gather x1, waiting for transfers between devices, shards(): whole_rows = lax.all_gather(token_rows, VOCAB, axis=1, tiled=True)  68.8 us
    psum x4, blocking collectives, by_axis_2(): shard = lax.psum(shard, axis)  60.1 us
    pmax x4, blocking collectives, by_axis(): shard = lax.pmax(shard, axis)  39.7 us
    all_gather x1, blocking collectives, shards(): seq_rows = lax.all_gather(hidden, 'ctx', axis=1, tiled=True)  26.5 us
    dot_general x1, matrix products, contract_rows(): lax.dot_general(block_rows, both_logits, (((0,), (0,)), ((), ())), prefer...  20.1 us
    all_gather x1, blocking collectives, gather_packed(): lines, at, finished = (lax.all_gather(flat, axis), 0, [])  18.1 us
    dot_general x1, matrix products, shards(): jnp.dot(whole_rows, head_weight, preferred_element_type=jnp.float32)  14.8 us
  transfers between devices with their start and end apart: 1, of which 1 were waited for; matrix products, arithmetic and copies ran while one was open for 1% of the time, Pallas kernels for 0%

commit v1 on v0

v1 whole, which is shorter than its diff:
```python
import functools

import jax
import jax.numpy as jnp
from jax import lax
from jax.experimental import pallas as pl
from jax.experimental.pallas import tpu as pltpu
from jax.sharding import Mesh
from jax.sharding import PartitionSpec as P

V = 128256
NX, NY, NZ, NC = 4, 4, 8, 2
AX, AY, AZ, AC = "vocab_1", "vocab_0", "ctx", "vocab_2"
VOCAB = (AY, AX, AC)
CTX_VOCAB = (AZ,) + VOCAB
MESH = pl.DeviceIdType.MESH

SEQS = 16
PER = 4
CHUNKS = SEQS // PER
PAIRS = SEQS // 2
ROWS = 16
LENGTH = ROWS * NZ
LANES = 128
CHIPS = NX * NY
WIDTH = 501
PAD = 512

strength = 0.1
loss_scale = 256.0


def kind_of(s):
    q, j = divmod(s, PER)
    if j == 2:
        return "z"
    if j == 3:
        return "x" if q % 2 == 0 else "y"
    return "xy"[j]


def kernel(
    hid_ref, w_hbm, ids_ref, mask_ref, order_ref, frozen_ref,
    loss_ref, margins_ref, head_hbm, spread_hbm,
    held, w_ref, acc, logits, both, staged, meta, stats, cols, masks, turn,
    w_sem, r1, r2, r3, s1, s2, s3, pair_r, pair_s, meta_r, meta_s, stat_r, stat_s, out_sem,
):
    x = lax.axis_index(AX)
    y = lax.axis_index(AY)
    z = lax.axis_index(AZ)
    c = lax.axis_index(AC)
    place = y * NX + x
    shard = ((z * NY + y) * NX + x) * NC + c

    w_copy = pltpu.make_async_copy(w_hbm, w_ref, w_sem)
    w_copy.start()

    def peer(axis, step):
        index, size = {AX: (x, NX), AY: (y, NY), AZ: (z, NZ), AC: (c, NC)}[axis]
        return {axis: lax.rem(index + step + size, size)}

    def send(ref, send_sem, recv_sem, to):
        pltpu.make_async_remote_copy(
            src_ref=ref, dst_ref=ref, send_sem=send_sem, recv_sem=recv_sem,
            device_id=to, device_id_type=MESH,
        ).start()

    def arrived(ref, sem):
        pltpu.make_async_copy(ref, ref, sem).wait()

    def across(ref, s):
        send(ref, pair_s.at[s // PER], pair_r.at[s // PER], peer(AC, 1))

    for j in range(SEQS):
        seq = order_ref[j // 2 + (j % 2) * PAIRS]
        held[j, place, c, pl.ds(z * ROWS, ROWS), :] = hid_ref[seq]
    turn[...] = jnp.zeros_like(turn)
    for j in range(SEQS):
        seq = order_ref[j // 2 + (j % 2) * PAIRS]
        turn[pl.ds(j, 1), 0:ROWS] = ids_ref[pl.ds(seq, 1), :].astype(jnp.float32)
        turn[pl.ds(SEQS + j, 1), 0:ROWS] = mask_ref[pl.ds(seq, 1), :].astype(jnp.float32)
    meta[pl.ds(z * ROWS, ROWS), :] = turn[...].T[0:ROWS, :]

    barrier = pltpu.get_barrier_semaphore()
    greeted = 0
    for axis, size in ((AX, NX), (AY, NY), (AZ, NZ), (AC, NC)):
        for step in range(1, size):
            pl.semaphore_signal(barrier, inc=1, device_id=peer(axis, step), device_id_type=MESH)
            greeted += 1
    pl.semaphore_wait(barrier, greeted)

    def axes_of(s):
        return (AY, AX) if kind_of(s) == "x" else (AX, AY)

    def line(s, i2, i3):
        if kind_of(s) == "x":
            row, col = lax.rem(y + i2, NY), lax.rem(x + i3, NX)
        else:
            row, col = lax.rem(y + i3, NY), lax.rem(x + i2, NX)
        return held.at[s, row * NX + col, c]

    def half(ref, side):
        return ref.at[pl.ds(side * (LENGTH // 2), LENGTH // 2), :]

    def own_rows(step=0):
        return pl.ds(lax.rem(z + step + NZ, NZ) * ROWS, ROWS)

    def bar(s, i2, side=None):
        row = lax.rem(y + i2, NY) * NX
        if side is None:
            return held.at[s, pl.ds(row, NX), c, own_rows(), :]
        return held.at[s, pl.ds(row + side * 2, 2), c, own_rows(), :]

    def plane(s, i3, side=None):
        if side is None:
            return held.at[s, :, c, own_rows(i3), :]
        return held.at[s, pl.ds(side * (CHIPS // 2), CHIPS // 2), c, own_rows(i3), :]

    def third(s, k):
        a3 = axes_of(s)[1]
        ref = line(s, k, 0)
        send(ref, s3.at[s], r3.at[s, 4 * k], peer(a3, 1))
        send(ref, s3.at[s], r3.at[s, 4 * k + 1], peer(a3, -1))
        across(ref, s)

    def round_a(s):
        ref = held.at[s, place, c, own_rows(), :]
        axis, size = (AX, NX) if kind_of(s) == "z" else (AZ, NZ)
        for step in range(1, size):
            send(ref, s1.at[s], r1.at[s], peer(axis, step))

    def round_b(s):
        if kind_of(s) == "z":
            arrived(held.at[s, 0, 0, pl.ds(0, (NX - 1) * ROWS), :], r1.at[s])
            ref = bar(s, 0)
            send(ref, s2.at[s], r2.at[s, 0], peer(AY, 1))
            send(ref, s2.at[s], r2.at[s, 1], peer(AY, -1))
        else:
            arrived(held.at[s, 0, 0, pl.ds(0, (NZ - 1) * ROWS), :], r1.at[s])
            a2 = axes_of(s)[0]
            ref = line(s, 0, 0)
            send(ref, s2.at[s], r2.at[s, 0], peer(a2, 1))
            send(ref, s2.at[s], r2.at[s, 1], peer(a2, -1))
            third(s, 0)

    def round_c(s):
        if kind_of(s) == "z":
            arrived(bar(s, 3), r2.at[s, 0])
            send(bar(s, 3, 0), s2.at[s], r2.at[s, 2], peer(AY, 1))
            arrived(bar(s, 1), r2.at[s, 1])
            send(bar(s, 1, 1), s2.at[s], r2.at[s, 3], peer(AY, -1))
        else:
            a2 = axes_of(s)[0]
            arrived(line(s, 3, 0), r2.at[s, 0])
            send(half(line(s, 3, 0), 0), s2.at[s], r2.at[s, 2], peer(a2, 1))
            third(s, 3)
            arrived(line(s, 1, 0), r2.at[s, 1])
            send(half(line(s, 1, 0), 1), s2.at[s], r2.at[s, 3], peer(a2, -1))
            third(s, 1)

    def round_d(s):
        if kind_of(s) == "z":
            arrived(bar(s, 2, 0), r2.at[s, 2])
            arrived(bar(s, 2, 1), r2.at[s, 3])
            ref = plane(s, 0)
            send(ref, s3.at[s], r3.at[s, 0], peer(AZ, 1))
            send(ref, s3.at[s], r3.at[s, 4], peer(AZ, -1))
            across(ref, s)
        else:
            arrived(half(line(s, 2, 0), 0), r2.at[s, 2])
            arrived(half(line(s, 2, 0), 1), r2.at[s, 3])
            third(s, 2)

    def ring_of_four(s, k):
        a3 = axes_of(s)[1]
        arrived(line(s, k, 3), r3.at[s, 4 * k])
        send(half(line(s, k, 3), 0), s3.at[s], r3.at[s, 4 * k + 2], peer(a3, 1))
        across(line(s, k, 3), s)
        arrived(line(s, k, 1), r3.at[s, 4 * k + 1])
        send(half(line(s, k, 1), 1), s3.at[s], r3.at[s, 4 * k + 3], peer(a3, -1))
        across(line(s, k, 1), s)

    def ring_of_eight(s, d):
        left, right = plane(s, -d), plane(s, d)
        arrived(left, r3.at[s, d - 1])
        send(left if d < 3 else plane(s, -d, 0), s3.at[s], r3.at[s, d], peer(AZ, 1))
        across(left, s)
        arrived(right, r3.at[s, 3 + d])
        send(right if d < 3 else plane(s, d, 1), s3.at[s], r3.at[s, 4 + d], peer(AZ, -1))
        across(right, s)

    def round_e(s):
        if kind_of(s) == "z":
            ring_of_eight(s, 1)
        else:
            ring_of_four(s, 0)

    def round_f(s):
        if kind_of(s) == "z":
            ring_of_eight(s, 2)
        else:
            ring_of_four(s, 3)
            ring_of_four(s, 1)

    def round_g(s):
        if kind_of(s) == "z":
            ring_of_eight(s, 3)
        else:
            ring_of_four(s, 2)

    def round_h(s):
        if kind_of(s) == "z":
            arrived(plane(s, 4, 0), r3.at[s, 3])
            arrived(plane(s, 4, 1), r3.at[s, 7])
            across(plane(s, 4), s)
        else:
            for k in (0, 3, 1, 2):
                arrived(half(line(s, k, 2), 0), r3.at[s, 4 * k + 2])
                arrived(half(line(s, k, 2), 1), r3.at[s, 4 * k + 3])
                across(line(s, k, 2), s)

    def chunk(q, step):
        if q < CHUNKS:
            for j in (2, 0, 1, 3):
                step(q * PER + j)

    def forward(q):
        @pl.loop(0, PER // 2)
        def _(i):
            s = q * PER + i * 2
            total = jnp.zeros((2 * LENGTH, WIDTH), jnp.float32)
            for k in range(CHIPS):
                lhs = jnp.concatenate(
                    [held[pl.ds(s, 2), k, e].reshape(2 * LENGTH, LANES) for e in range(NC)], axis=1
                )
                total += jnp.dot(
                    lhs, w_ref[pl.ds(k * NC * LANES, NC * LANES), :], preferred_element_type=jnp.float32
                )
            logits[pl.ds(s, 2)] = total.reshape(2, LENGTH, WIDTH)

    lane = lax.broadcasted_iota(jnp.int32, (LENGTH, LANES), 1)
    column = (lax.broadcasted_iota(jnp.int32, (LENGTH, WIDTH), 1) + shard * WIDTH).astype(jnp.float32)

    def local_stats(q):
        table = jnp.zeros((LENGTH, LANES), jnp.float32)
        for j in range(PER):
            s = q * PER + j
            part = logits[s]
            top = jnp.max(part, axis=1, keepdims=True)
            total = jnp.sum(jnp.exp(part - top), axis=1, keepdims=True)
            hit = column == meta[:, s : s + 1]
            target = jnp.sum(jnp.where(hit, part, 0.0), axis=1, keepdims=True)
            table = jnp.where(lane == j, top, table)
            table = jnp.where(lane == 8 + j, total, table)
            table = jnp.where(lane == 16 + j, target, table)
        return table.T[0:24, :]

    stages = ((AC, c, NC, 0), (AX, x, NX, 2), (AY, y, NY, 6), (AZ, z, NZ, 10))

    def share(q, stage, value):
        axis, index, size, at = stages[stage]
        ref = stats.at[q, at + index]
        ref[...] = value
        for step in range(1, size):
            send(ref, stat_s.at[q, stage], stat_r.at[q, stage], peer(axis, step))

    def merged(q, stage):
        axis, index, size, at = stages[stage]
        arrived(stats.at[q, pl.ds(0, size - 1)], stat_r.at[q, stage])
        parts = [stats[q, at + i] for i in range(size)]
        top = functools.reduce(jnp.maximum, [p[0:8] for p in parts])
        total = sum(p[8:16] * jnp.exp(p[0:8] - top) for p in parts)
        target = sum(p[16:24] for p in parts)
        return top, total, target

    def relay(q, stage):
        share(q, stage + 1, jnp.concatenate(merged(q, stage), axis=0))

    row8 = lax.broadcasted_iota(jnp.int32, (8, LANES), 0)

    def coefs(q, loss):
        top, total, target = merged(q, 3)
        log_norm = top + jnp.log(total)
        mask = masks[q]
        frozen = jnp.zeros((8, LANES), jnp.float32)
        for j in range(PER):
            seq = order_ref[q * 2 + j // 2 + (j % 2) * PAIRS]
            frozen = jnp.where(row8 == j, frozen_ref[seq], frozen)
        terms = jnp.where(row8 < PER, (target - log_norm) * mask, 0.0)
        ratio = jnp.sum(terms, axis=1, keepdims=True) - frozen
        even = row8 % 2 == 0
        after = jnp.concatenate([ratio[1:8], ratio[0:1]], axis=0)
        before = jnp.concatenate([ratio[7:8], ratio[0:7]], axis=0)
        margin = strength * jnp.where(even, ratio - after, before - ratio)
        tail = jnp.exp(-jnp.abs(margin))
        soft = jnp.maximum(-margin, 0.0) + jnp.log1p(tail)
        sigmoid = jnp.where(margin > 0, tail, 1.0) / (1.0 + tail)
        weight = -loss_scale * strength * sigmoid / PAIRS
        coef = jnp.where(even, weight, -weight) * mask
        for i in range(PER // 2):
            margins_ref[q * 2 + i] = jnp.max(margin[2 * i : 2 * i + 1, 0:1])
            loss = loss + jnp.max(soft[2 * i : 2 * i + 1, 0:1])
        table = jnp.concatenate(
            [log_norm, coef, jnp.zeros((LANES - 16, LANES), jnp.float32)], axis=0
        )
        cols[...] = table.T
        for j in range(PER):
            s = q * PER + j
            prob = jnp.exp(logits[s] - cols[:, j : j + 1])
            weight_col = cols[:, 8 + j : 9 + j]
            onehot = jnp.where(column == meta[:, s : s + 1], 1.0, 0.0)
            rows = pl.ds(j * LENGTH, LENGTH)
            both[rows, 0:WIDTH] = (weight_col * (onehot - prob)).astype(jnp.bfloat16)
            both[rows, PAD : PAD + WIDTH] = ((V / 64.0) * weight_col * prob).astype(jnp.bfloat16)
        return loss

    def backward(q, first, last):
        @pl.loop(first, last)
        def _(k):
            lhs = jnp.concatenate(
                [held[pl.ds(q * PER, PER), k, e].reshape(PER * LENGTH, LANES) for e in range(NC)], axis=1
            )
            part = lax.dot_general(
                lhs, both[...], (((0,), (0,)), ((), ())), preferred_element_type=jnp.float32
            )
            if q > 0:
                part = part + acc[k]
            if q < CHUNKS - 1:
                acc[k] = part
            else:
                rows = pl.ds(k * NC * LANES, NC * LANES)
                staged[0, k] = part[:, 0:WIDTH].astype(jnp.bfloat16)
                staged[1, k] = part[:, PAD : PAD + WIDTH].astype(jnp.bfloat16)
                pltpu.make_async_copy(staged.at[0, k], head_hbm.at[rows, :], out_sem.at[0]).start()
                pltpu.make_async_copy(staged.at[1, k], spread_hbm.at[rows, :], out_sem.at[1]).start()

    chunk(0, round_a)
    own_meta = meta.at[own_rows(), :]
    for step in range(1, NZ):
        send(own_meta, meta_s, meta_r, peer(AZ, step))
    chunk(1, round_a)
    both[...] = jnp.zeros_like(both)
    chunk(0, round_b)
    chunk(0, round_c)
    chunk(0, round_d)
    arrived(meta.at[pl.ds(0, (NZ - 1) * ROWS), :], meta_r)
    turned = meta[...].T
    for q in range(CHUNKS):
        rows = turned[SEQS + q * PER : SEQS + (q + 1) * PER]
        masks[q] = jnp.concatenate([rows, jnp.zeros((8 - PER, LANES), jnp.float32)], axis=0)
    w_copy.wait()
    loss = jnp.float32(0.0)
    for q in range(CHUNKS):
        chunk(q + 2, round_a)
        chunk(q + 1, round_b)
        chunk(q, round_e)
        if q > 0:
            relay(q - 1, 0)
        if q == 3:
            backward(0, 0, 6)
        chunk(q + 1, round_c)
        chunk(q, round_f)
        if q > 0:
            relay(q - 1, 1)
        if q == 3:
            backward(0, 6, 11)
        chunk(q + 1, round_d)
        chunk(q, round_g)
        if q > 0:
            relay(q - 1, 2)
        if q == 3:
            backward(0, 11, CHIPS)
        chunk(q, round_h)
        arrived(held.at[pl.ds(q * PER, PER), :, 0], pair_r.at[q])
        forward(q)
        share(q, 0, local_stats(q))
        if q == 1:
            loss = coefs(0, loss)
    loss = coefs(1, loss)
    relay(3, 0)
    backward(1, 0, 9)
    relay(3, 1)
    backward(1, 9, CHIPS)
    loss = coefs(2, loss)
    backward(2, 0, 2)
    relay(3, 2)
    backward(2, 2, CHIPS)
    loss = coefs(3, loss)
    backward(3, 0, CHIPS)
    loss_ref[0] = loss / PAIRS

    for s in range(SEQS):
        first = (NX if kind_of(s) == "z" else NZ) - 1
        arrived(held.at[s, 0, 0, pl.ds(0, first * ROWS), :], s1.at[s])
        if kind_of(s) == "z":
            arrived(held.at[s, pl.ds(0, 3), 0, pl.ds(0, LENGTH // 2), :], s2.at[s])
            arrived(held.at[s, pl.ds(0, 14), 0], s3.at[s])
        else:
            arrived(held.at[s, pl.ds(0, 3), 0], s2.at[s])
            arrived(held.at[s, pl.ds(0, 12), 0], s3.at[s])
    for q in range(CHUNKS):
        arrived(held.at[pl.ds(q * PER, PER), :, 0], pair_s.at[q])
        for stage in range(4):
            arrived(stats.at[q, pl.ds(0, stages[stage][2] - 1)], stat_s.at[q, stage])
    arrived(meta.at[pl.ds(0, (NZ - 1) * ROWS), :], meta_s)
    for i in range(2):
        arrived(staged.at[i], out_sem.at[i])


def shards(hidden, head_weight, token_ids, response_mask, pair_order, frozen_logprob):
    depth = head_weight.shape[0]
    vmem = pl.BlockSpec(memory_space=pltpu.VMEM)
    smem = pl.BlockSpec(memory_space=pltpu.SMEM)
    hbm = pl.BlockSpec(memory_space=pl.ANY)
    dma = pltpu.SemaphoreType.DMA
    loss, margins, head_grad, spread_grad = pl.pallas_call(
        kernel,
        out_shape=(
            jax.ShapeDtypeStruct((1,), jnp.float32),
            jax.ShapeDtypeStruct((PAIRS,), jnp.float32),
            jax.ShapeDtypeStruct((depth, WIDTH), jnp.bfloat16),
            jax.ShapeDtypeStruct((depth, WIDTH), jnp.bfloat16),
        ),
        in_specs=[vmem, hbm, vmem, vmem, smem, smem],
        out_specs=(smem, smem, hbm, hbm),
        scratch_shapes=[
            pltpu.VMEM((SEQS, CHIPS, NC, LENGTH, LANES), jnp.bfloat16),
            pltpu.VMEM((depth, WIDTH), jnp.bfloat16),
            pltpu.VMEM((CHIPS, NC * LANES, 2 * PAD), jnp.float32),
            pltpu.VMEM((SEQS, LENGTH, WIDTH), jnp.float32),
            pltpu.VMEM((PER * LENGTH, 2 * PAD), jnp.bfloat16),
            pltpu.VMEM((2, CHIPS, NC * LANES, WIDTH), jnp.bfloat16),
            pltpu.VMEM((LENGTH, LANES), jnp.float32),
            pltpu.VMEM((CHUNKS, 18, 24, LANES), jnp.float32),
            pltpu.VMEM((LENGTH, LANES), jnp.float32),
            pltpu.VMEM((CHUNKS, 8, LANES), jnp.float32),
            pltpu.VMEM((LANES, LANES), jnp.float32),
            dma,
            dma((SEQS,)),
            dma((SEQS, 4)),
            dma((SEQS, 16)),
            dma((SEQS,)),
            dma((SEQS,)),
            dma((SEQS,)),
            dma((CHUNKS,)),
            dma((CHUNKS,)),
            dma,
            dma,
            dma((CHUNKS, 4)),
            dma((CHUNKS, 4)),
            dma((2,)),
        ],
        compiler_params=pltpu.CompilerParams(
            collective_id=0, has_side_effects=True, vmem_limit_bytes=62 * 1024 * 1024
        ),
    )(hidden, head_weight, token_ids, response_mask, pair_order, frozen_logprob)
    return loss.reshape(()), margins, head_grad, spread_grad


def solution(mesh):
    split = Mesh(mesh.devices.reshape(NZ, NY, NX, NC), CTX_VOCAB)
    placed = (P(None, AZ, VOCAB), P(None, CTX_VOCAB), P(None, AZ), P(None, AZ), P(), P())
    return jax.shard_map(
        shards,
        mesh=split,
        in_specs=placed,
        out_specs=(P(), P(), P(None, CTX_VOCAB), P(None, CTX_VOCAB)),
        check_vma=False,
    )
```

time: 282 us -> 147 us (0.52)
  blocking collectives: 144 us -> 0 us
  Pallas kernels: 0 us -> 124 us
  waiting for transfers between devices: 68.8 us -> 0 us
  matrix products: 34.9 us -> 0 us
  between operations: 15.9 us -> 2.4 us
  local copies, waits for them, and re-layouts: 8.6 us -> 19.6 us
  other arithmetic: 8.44 us -> 0 us
    pallas_call x0 -> x1, Pallas kernels: none -> 124 us  [shards(): pl.pallas_call(kernel, out_shape=(jax.ShapeDtypeStruct((1,), jnp.float32)...]
    all_gather x1 -> x0, waiting for transfers between devices: 68.8 us -> none  [shards(): whole_rows = lax.all_gather(token_rows, VOCAB, axis=1, tiled=True)]
    psum x4 -> x0, blocking collectives: 60.1 us -> none  [by_axis_2(): shard = lax.psum(shard, axis)]
    all_gather x2 -> x0, blocking collectives: 44.6 us -> none  [the longest x1 26.5 us: shards(): seq_rows = lax.all_gather(hidden, 'ctx', axis=1, tiled=True)]
    pmax x4 -> x0, blocking collectives: 39.7 us -> none  [by_axis(): shard = lax.pmax(shard, axis)]
    dot_general x2 -> x0, matrix products: 34.9 us -> none  [the longest x1 20.1 us: contract_rows(): lax.dot_general(block_rows, both_logits, (((0,), (0,)), ((), ())), prefer...]
    unnamed x5 -> x6, local copies, waits for them, and re-layouts: 0.01 us -> 19.6 us
    slice x1 -> x0, local copies, waits for them, and re-layouts: 4 us -> none  [shards(): spread_grad = both_grads[:, shard_width:].astype(jnp.bfloat16)]
  transfers between devices with their start and end apart: 1 -> 0, of which waited for: 1 -> 0; matrix products, arithmetic and copies ran while one was open for 1% -> 0% of each run, Pallas kernels for 0% -> 0%
where the time goes in v1:
time: 147 us; the launch traced here: 146 us
  Pallas kernels  124 us (84%)
  local copies, waits for them, and re-layouts  19.6 us (13%)
  between operations  2.4 us (2%)
    pallas_call x1, Pallas kernels, shards(): pl.pallas_call(kernel, out_shape=(jax.ShapeDtypeStruct((1,), jnp.float32)...  124 us
    unnamed x6, local copies, waits for them, and re-layouts  19.6 us

profile of v1, /device:TPU:1, one launch (start us, length us, event | category | flops | bytes accessed | tf_op | source)
XLA Modules:
  0.0 146.4 jit_solution(12403082013861971318)
XLA Ops:
  0.6 6.5 %copy.10.w_hbm = bf16[4096,501]{1,0:T(8,128)(2,1)} copy(bf16[4096,501]{0,1:T(8,128)(2,1)} %param.7) | data formatting | bytes 8208384 | tf_op args[1]
  7.1 124.4 %shard_map.93 = (f32[1]{0:T(128)}, f32[8]{0:T(128)}, bf16[4096,501]{1,0:T(8,128)(2,1)}, bf16[4096,501]{1,0:T(8,128)(2,1)}) custom-call(bf16[16,16,128]{2,1,0:T(8,128)(2,1)} %hid_ref.1, bf16[4096,501]{1,0:T(8,128)(2,1)} %copy.10.w_hbm, s32[16,16]{1,0:T(8,128)} %ids_ref.1, s32[16,16]{1,0:T(8,128)} %mask_ref.1, s32[16]{0:T(128)} %order_ref.1, f32[16]{0:T(128)} %frozen_ref.1), custom_call_target="tpu_custom_call" | custom-call | tf_op jit(solution)/shard_map/pallas_call | solution.py:416
  131.5 6.3 %copy.11 = bf16[4096,501]{0,1:T(8,128)(2,1)} copy(bf16[4096,501]{1,0:T(8,128)(2,1)} %get-tuple-element.14) | data formatting | bytes 8208384
  137.9 0.0 copy-start
  137.9 6.3 %copy.12 = bf16[4096,501]{0,1:T(8,128)(2,1)} copy(bf16[4096,501]{1,0:T(8,128)(2,1)} %get-tuple-element.15) | data formatting | bytes 8208384
  144.8 0.0 copy-done
  144.8 0.5 copy.16
Async XLA Ops:
  137.9 6.9 %copy-start = (f32[8]{0:T(128)S(1)}, f32[8]{0:T(128)}, u32[]{:S(2)}) copy-start(f32[8]{0:T(128)} %get-tuple-element.21) | copy-start | bytes 100
